TPU v7x, 32 devices: a whole 2x2x4 slice. The times are simulated.
32 devices in a mesh: groups: 2 (over y), blk: 4 (over z), tile: 2 (over x), sub: 2 (over core).
Axes of the slice: x: 2, y: 2, z: 4, core: 2. Of those that a mesh axis runs over, the one named last changes fastest.
Arguments:
- raw_desc: bfloat16 [4096, 1536], P(('groups', 'blk', 'tile')), parts along dimension 0, may hold values from -11 to 11
- desc_mean: float32 [1536], replicated, may hold values from -6 to 6
- whitening: bfloat16 [1536, 256], P(None, 'sub'), may hold values from -0.15625 to 0.15625
Outputs:
- augmented: float32 [4096, 256], P(('groups', 'blk', 'tile'), 'sub'), parts along dimension 0
There are 2 independent parts, one for each index of `groups`. A program takes and returns all parts, laid end to end along the dimension named above; an argument that names none is the same for every part. Nothing has to cross between parts.
All inputs are finite; a program needn't handle non-finite values.
Results may differ from a plain program's by a relative error of at most 0.0055.
The roundings to bfloat16 on the way count: a program that leaves them out, or rounds other values in their place, can miss the bound.
Values may be sent and summed in bfloat16 or wider, within the bound.
A program may use at most 128 MiB of HBM per device.

v0:
```python
import functools

import jax
import jax.numpy as jnp
from jax import lax
from jax.experimental import pallas as pl
from jax.experimental.pallas import tpu as pltpu
from jax.sharding import PartitionSpec as P

beta = 0.125
lowest = -1e30
MESH = pl.DeviceIdType.MESH


def repeat(count, body):
    if count <= 8:
        for k in range(count):
            body(k)
    else:
        lax.fori_loop(0, count, lambda k, _: (body(k), 0)[1], 0)


def peer_of(me, k, count):
    if count == 4:
        if k == 0:
            return me + 1 - 2 * lax.rem(me, 2)
        if k == 1:
            return lax.rem(me + 2, 4)
        return 3 - me
    return lax.rem(me + k + 1, count)


def kernel(
    blks, tiles, chunks,
    raw_hbm, mean_ref, white_hbm, out_ref,
    raw, white, feats, keys, acc, stat, put_acc, put_stat, got_acc, got_stat,
    raw_sem, white_sem, pair_send, pair_recv, own_send, fwd_send, key_recv,
    part_send, part_recv,
):
    z, x, s = lax.axis_index("blk"), lax.axis_index("tile"), lax.axis_index("sub")
    other = 1 - s
    rows, width = feats.shape[1], feats.shape[2]
    part = rows // 2
    step = rows // chunks
    load_white = pltpu.make_async_copy(white_hbm, white, white_sem)
    load_white.start()
    loads = []
    for c in range(chunks):
        at = pl.ds(c * step, step)
        loads.append(pltpu.make_async_copy(raw_hbm.at[at], raw.at[at], raw_sem.at[c]))
        loads[-1].start()

    barrier = pltpu.get_barrier_semaphore()
    pl.semaphore_signal(barrier, inc=1, device_id={"sub": other}, device_id_type=MESH)

    def greet_z(k):
        for r in range(2):
            pl.semaphore_signal(
                barrier, inc=1, device_id={"blk": peer_of(z, k, blks), "sub": r},
                device_id_type=MESH,
            )

    def greet_x(k):
        for r in range(2):
            pl.semaphore_signal(
                barrier, inc=1, device_id={"tile": peer_of(x, k, tiles), "sub": r},
                device_id_type=MESH,
            )

    repeat(blks - 1, greet_z)
    repeat(tiles - 1, greet_x)

    def piece(r):
        return feats.at[s, pl.ds(r * part, part)]

    def slot(zz, xx):
        return zz * tiles + xx

    def own_to_z(k, r):
        return pltpu.make_async_remote_copy(
            piece(r), keys.at[slot(z, x), s], own_send.at[k, r], key_recv.at[slot(z, x), s],
            device_id={"blk": peer_of(z, k, blks), "sub": r}, device_id_type=MESH,
        )

    def own_to_x(k, r):
        return pltpu.make_async_remote_copy(
            piece(r), keys.at[slot(z, x), s], own_send.at[blks - 1 + k, r],
            key_recv.at[slot(z, x), s],
            device_id={"tile": peer_of(x, k, tiles), "sub": r}, device_id_type=MESH,
        )

    def forward(k, j, h):
        block = slot(peer_of(z, k, blks), x)
        return pltpu.make_async_remote_copy(
            keys.at[block, h], keys.at[block, h], fwd_send.at[k, j, h],
            key_recv.at[block, h],
            device_id={"tile": peer_of(x, j, tiles)}, device_id_type=MESH,
        )

    def pair(r):
        return pltpu.make_async_remote_copy(
            piece(r), piece(r), pair_send.at[r], pair_recv.at[r],
            device_id={"sub": other}, device_id_type=MESH,
        )

    mean = mean_ref[...].reshape(1, -1)
    load_white.wait()
    for c in range(chunks):
        loads[c].wait()
        at = pl.ds(c * step, step)
        centred = (raw[at, :].astype(jnp.float32) - mean).astype(jnp.bfloat16)
        half = jnp.dot(centred, white[...], preferred_element_type=jnp.float32)
        feats[s, at, :] = half.astype(jnp.bfloat16)
        if (c + 1) % (chunks // 2) == 0:
            r = (c + 1) // (chunks // 2) - 1
            if r == 0:
                pl.semaphore_wait(barrier, 1 + 2 * (blks - 1) + 2 * (tiles - 1))
            repeat(blks - 1, lambda k: own_to_z(k, r).start())
            repeat(tiles - 1, lambda k: own_to_x(k, r).start())
            pair(r).start()

    def arrived(block, h):
        pltpu.make_async_copy(
            keys.at[block, h], keys.at[block, h], key_recv.at[block, h]
        ).wait()

    def scores_of(k0, k1):
        nt = (((1,), (1,)), ((), ()))
        q = jnp.concatenate([feats[0], feats[1]], axis=1)
        kk = jnp.concatenate([k0, k1], axis=1)
        return beta * lax.dot_general(q, kk, nt, preferred_element_type=jnp.float32), kk

    def attend(block):
        sc, kk = scores_of(keys[block, 0], keys[block, 1])
        old = stat[0]
        top = jnp.maximum(old, jnp.max(sc, axis=1, keepdims=True))
        scale = jnp.exp(old - top)
        expo = jnp.exp(sc - top[:, :1])
        stat[0] = top
        stat[1] = stat[1] * scale + jnp.sum(expo, axis=1, keepdims=True)
        acc[...] = acc[...] * scale[:, :1] + jnp.dot(
            expo.astype(jnp.bfloat16), kk, preferred_element_type=jnp.float32
        )

    for r in range(2):
        pair(r).wait()
    mine = pl.ds(pl.multiple_of(s * part, part), part)
    sc, kk = scores_of(feats[0, mine, :], feats[1, mine, :])
    query = lax.broadcasted_iota(jnp.int32, sc.shape, 0)
    key = lax.broadcasted_iota(jnp.int32, sc.shape, 1) + s * part
    masked = query == key
    sc = jnp.where(masked, lowest, sc)
    top = jnp.max(sc, axis=1, keepdims=True)
    expo = jnp.where(masked, 0.0, jnp.exp(sc - top))
    stat[0] = jnp.broadcast_to(top, stat.shape[1:])
    stat[1] = jnp.broadcast_to(jnp.sum(expo, axis=1, keepdims=True), stat.shape[1:])
    acc[...] = jnp.dot(expo.astype(jnp.bfloat16), kk, preferred_element_type=jnp.float32)

    def from_z(k):
        block = slot(peer_of(z, k, blks), x)
        for h in range(2):
            arrived(block, h)
            repeat(tiles - 1, lambda j: forward(k, j, h).start())
        attend(block)

    def from_x(k):
        block = slot(z, peer_of(x, k, tiles))
        for h in range(2):
            arrived(block, h)
        attend(block)

    def diagonal(k):
        def one(j):
            block = slot(peer_of(z, k, blks), peer_of(x, j, tiles))
            for h in range(2):
                arrived(block, h)
            attend(block)
        repeat(tiles - 1, one)

    repeat(tiles - 1, from_x)
    repeat(blks - 1, from_z)
    repeat(blks - 1, diagonal)

    put_acc[...] = acc[...].astype(jnp.bfloat16)
    lane = lax.broadcasted_iota(jnp.int32, put_stat.shape, 1)
    put_stat[...] = jnp.where(lane < width // 2, stat[0], stat[1])
    send_acc = pltpu.make_async_remote_copy(
        put_acc, got_acc, part_send.at[0], part_recv.at[0],
        device_id={"sub": other}, device_id_type=MESH,
    )
    send_stat = pltpu.make_async_remote_copy(
        put_stat, got_stat, part_send.at[1], part_recv.at[1],
        device_id={"sub": other}, device_id_type=MESH,
    )
    send_stat.start()
    send_acc.start()

    def own_sent(k):
        for r in range(2):
            own_to_z(k, r).wait_send()

    def own_sent_x(k):
        for r in range(2):
            own_to_x(k, r).wait_send()

    def fwd_sent(k):
        def one(j):
            for h in range(2):
                forward(k, j, h).wait_send()
        repeat(tiles - 1, one)

    repeat(blks - 1, own_sent)
    repeat(tiles - 1, own_sent_x)
    repeat(blks - 1, fwd_sent)

    send_stat.wait()
    my_top, my_total = stat[0][:, :1], stat[1][:, :1]
    its_top, its_total = got_stat[:, :1], got_stat[:, width // 2:width // 2 + 1]
    top = jnp.maximum(my_top, its_top)
    mine_by, its_by = jnp.exp(my_top - top), jnp.exp(its_top - top)
    total = my_total * mine_by + its_total * its_by
    mine_by, its_by = mine_by / total, its_by / total
    send_acc.wait()
    gathered = acc[...] * mine_by + got_acc[...].astype(jnp.float32) * its_by
    whole = jnp.concatenate([feats[0], feats[1]], axis=1).astype(jnp.float32)
    mixed = whole + gathered
    squares = jnp.sum(mixed * mixed, axis=1, keepdims=True)
    wanted = jnp.where(s == 0, mixed[:, :width], mixed[:, width:])
    out_ref[...] = wanted * lax.rsqrt(squares + 1e-06)


def local(raw_desc, desc_mean, whitening):
    rows, depth = raw_desc.shape
    width = whitening.shape[1]
    blks, tiles = lax.axis_size("blk"), lax.axis_size("tile")
    chunks = 4
    part = rows // 2
    chips = blks * tiles
    vmem = pl.BlockSpec(memory_space=pltpu.VMEM)
    hbm = pl.BlockSpec(memory_space=pltpu.HBM)
    dma = pltpu.SemaphoreType.DMA
    bf16, f32 = jnp.bfloat16, jnp.float32
    raw_desc = pltpu.with_memory_space_constraint(raw_desc, pltpu.HBM)
    whitening = pltpu.with_memory_space_constraint(whitening, pltpu.HBM)
    return pl.pallas_call(
        functools.partial(kernel, blks, tiles, chunks),
        out_shape=jax.ShapeDtypeStruct((rows, width), f32),
        in_specs=[hbm, vmem, hbm],
        out_specs=vmem,
        scratch_shapes=[
            pltpu.VMEM((rows, depth), bf16),
            pltpu.VMEM((depth, width), bf16),
            pltpu.VMEM((2, rows, width), bf16),
            pltpu.VMEM((chips, 2, part, width), bf16),
            pltpu.VMEM((rows, 2 * width), f32),
            pltpu.VMEM((2, rows, width), f32),
            pltpu.VMEM((rows, 2 * width), bf16),
            pltpu.VMEM((rows, width), f32),
            pltpu.VMEM((rows, 2 * width), bf16),
            pltpu.VMEM((rows, width), f32),
            dma((chunks,)),
            dma,
            dma((2,)),
            dma((2,)),
            dma((blks - 1 + tiles - 1, 2)),
            dma((blks - 1, tiles - 1, 2)),
            dma((chips, 2)),
            dma((2,)),
            dma((2,)),
        ],
        compiler_params=pltpu.CompilerParams(collective_id=0, has_side_effects=True, vmem_limit_bytes=40 * 2 ** 20),
        name="augment",
    )(raw_desc, desc_mean, whitening)


def solution(mesh):
    return jax.shard_map(
        local,
        mesh=mesh,
        in_specs=(P(("groups", "blk", "tile"), None), P(), P(None, "sub")),
        out_specs=P(("groups", "blk", "tile"), "sub"),
        check_vma=False,
    )
```

profile of v0, /device:TPU:0, one launch (start us, length us, event | category | flops | bytes accessed | tf_op | source)
XLA Modules:
  0.0 19.1 jit_solution(12136667650400405090)
XLA Ops:
  0.0 0.0 copy-start
  0.0 0.7 %copy-done = f32[1536]{0:T(1024)S(1)} copy-done((f32[1536]{0:T(1024)S(1)}, f32[1536]{0:T(1024)}, u32[]{:S(2)}) %copy-start) | copy-done | bytes 6168
  0.7 17.8 %augment.1 = f32[256,128]{1,0:T(8,128)S(1)} custom-call(bf16[256,1536]{1,0:T(8,128)(2,1)} %raw_hbm.1, f32[1536]{0:T(1024)S(1)} %copy-done, bf16[1536,128]{1,0:T(8,128)(2,1)} %white_hbm.1), custom_call_target="tpu_custom_call" | custom-call | tf_op jit(solution)/shard_map/augment/pallas_call | solution.py:245
  18.5 0.7 %copy.5 = f32[256,128]{1,0:T(8,128)} copy(f32[256,128]{1,0:T(8,128)S(1)} %augment.1) | data formatting | bytes 262144
Async XLA Ops:
  0.0 0.7 %copy-start = (f32[1536]{0:T(1024)S(1)}, f32[1536]{0:T(1024)}, u32[]{:S(2)}) copy-start(f32[1536]{0:T(1024)} %mean_ref.1) | copy-start | bytes 18436
where the time goes:
time: 19.3 us; the launch traced here: 19.1 us
  Pallas kernels  17.8 us (92%)
  local copies, waits for them, and re-layouts  1.35 us (7%)
    pallas_call x1, Pallas kernels, local(): pl.pallas_call(functools.partial(kernel, blks, tiles, chunks), out_shape=...  17.8 us
    unnamed x3, local copies, waits for them, and re-layouts  1.35 us

commit v1 on v0

v1 whole, which is shorter than its diff:
```python
import functools

import jax
import jax.numpy as jnp
from jax import lax
from jax.experimental import pallas as pl
from jax.experimental.pallas import tpu as pltpu
from jax.sharding import PartitionSpec as P

beta = 0.125
lowest = -1e30
slabs = 3
pieces = 2
MESH = pl.DeviceIdType.MESH


def repeat(start, stop, body):
    if stop - start <= 8:
        for k in range(start, stop):
            body(k)
    else:
        lax.fori_loop(start, stop, lambda k, _: (body(k), 0)[1], 0)


def other_than(me, k):
    return k + jnp.where(k >= me, 1, 0)


def kernel(
    blks, tiles,
    raw_hbm, mean_hbm, white_hbm, out_ref,
    raw, mean, white, keys, acc, stat,
    raw_sem, white_sem, mean_sem, sent, recv, pair_recv, ready_z, ready_x, gone, token,
):
    z, x, s = lax.axis_index("blk"), lax.axis_index("tile"), lax.axis_index("sub")
    other = 1 - s
    rows, width = keys.shape[1], keys.shape[2]
    chips = blks * tiles
    piece = rows // pieces
    slab = raw.shape[1] // slabs
    load_mean = pltpu.make_async_copy(mean_hbm, mean, mean_sem)
    load_mean.start()
    loads = []
    for c in range(slabs):
        at = pl.ds(c * slab, slab)
        loads.append((
            pltpu.make_async_copy(white_hbm.at[at], white.at[at], white_sem.at[c]),
            pltpu.make_async_copy(raw_hbm.at[:, at], raw.at[:, at], raw_sem.at[c]),
        ))
        for load in loads[-1]:
            load.start()

    barrier = pltpu.get_barrier_semaphore()

    def to_z(k):
        return {"blk": other_than(z, k)}

    def to_x(k):
        return {"tile": other_than(x, k)}

    def greet(device):
        pl.semaphore_signal(barrier, inc=1, device_id=device, device_id_type=MESH)

    greet({"sub": other})

    def greet_z(k):
        @pl.when(k >= z)
        def _():
            greet(to_z(k))

    def greet_x(k):
        @pl.when(k >= x)
        def _():
            greet(to_x(k))

    def answer_z(k):
        @pl.when(k < z)
        def _():
            pl.semaphore_signal(ready_z.at[z - 1], inc=1, device_id=to_z(k), device_id_type=MESH)

    def answer_x(k):
        @pl.when(k < x)
        def _():
            pl.semaphore_signal(ready_x.at[x - 1], inc=1, device_id=to_x(k), device_id_type=MESH)

    repeat(0, blks - 1, greet_z)
    repeat(0, tiles - 1, greet_x)
    pl.semaphore_wait(barrier, 1 + z + x)
    repeat(0, blks - 1, answer_z)
    repeat(0, tiles - 1, answer_x)

    def slot(zz, xx):
        return zz * tiles + xx

    mine = slot(z, x)

    def send(block, p, device, done=sent):
        at = keys.at[2 * block + s, pl.ds(p * piece, piece)]
        pltpu.make_async_remote_copy(
            at, at, done, recv.at[block, p], device_id=device, device_id_type=MESH,
        ).start()

    def left_home(k):
        pltpu.make_async_copy(keys.at[0], keys.at[0], gone.at[k]).wait()

    def share(block, p):
        at = keys.at[2 * block + s, pl.ds(p * piece, piece)]
        pltpu.make_async_remote_copy(
            at, at, sent, pair_recv.at[block], device_id={"sub": other}, device_id_type=MESH,
        ).start()

    load_mean.wait()
    half = None
    for c in range(slabs):
        at = pl.ds(c * slab, slab)
        for load in loads[c]:
            load.wait()
        centred = (raw[:, at].astype(jnp.float32) - mean[at].reshape(1, -1)).astype(jnp.bfloat16)
        term = jnp.dot(centred, white[at, :], preferred_element_type=jnp.float32)
        half = term if half is None else half + term
    keys[2 * mine + s] = half.astype(jnp.bfloat16)
    def push(k):
        for p in range(pieces):
            send(mine, p, to_z(k), gone.at[k])

    def rightward(k):
        @pl.when(k >= z)
        def _():
            pl.semaphore_wait(ready_z.at[k], 1)
            push(k)

    def leftward(k):
        @pl.when(k < z - 1)
        def _():
            push(k)

    def sideward(k):
        @pl.when(k >= x)
        def _():
            pl.semaphore_wait(ready_x.at[k], 1)
        for p in range(pieces):
            send(mine, p, to_x(k))

    for p in range(pieces):
        share(mine, p)

    @pl.when(z > 0)
    def _():
        push(0)

    @pl.when(z > 1)
    def _():
        push(z - 1)

    repeat(0, tiles - 1, sideward)
    repeat(0, blks - 1, rightward)

    @pl.when((z > 1) & (z + 1 < blks))
    def _():
        left_home(0)
        for r in range(2):
            pl.semaphore_signal(
                token, inc=1, device_id={"blk": z + 1, "sub": r}, device_id_type=MESH,
            )

    @pl.when(z > 2)
    def _():
        pl.semaphore_wait(token, 2)
    repeat(1, blks - 1, leftward)

    def take(block, forward):
        for p in range(pieces):
            at = keys.at[2 * block + s, pl.ds(p * piece, piece)]
            pltpu.make_async_copy(at, at, recv.at[block, p]).wait()
            if forward:
                repeat(0, tiles - 1, lambda k: send(block, p, to_x(k)))
            share(block, p)

    def both(block):
        return jnp.concatenate([keys[2 * block], keys[2 * block + 1]], axis=1)

    def paired(block):
        at = keys.at[2 * block + other]
        pltpu.make_async_copy(at, at, pair_recv.at[block]).wait()

    def scores_of(kk):
        nt = (((1,), (1,)), ((), ()))
        return beta * lax.dot_general(both(mine), kk, nt, preferred_element_type=jnp.float32)

    def attend(*blocks):
        for block in blocks:
            paired(block)
        kk = jnp.concatenate([both(block) for block in blocks], axis=0)
        sc = scores_of(kk)
        old = stat[0]
        top = jnp.maximum(old, jnp.max(sc, axis=1, keepdims=True))
        scale = jnp.exp(old - top)
        expo = jnp.exp(sc - top[:, :1])
        stat[0] = top
        stat[1] = stat[1] * scale + jnp.sum(expo, axis=1, keepdims=True)
        acc[...] = acc[...] * scale[:, :1] + jnp.dot(
            expo.astype(jnp.bfloat16), kk, preferred_element_type=jnp.float32
        )

    paired(mine)
    kk = both(mine)
    sc = scores_of(kk)
    query = lax.broadcasted_iota(jnp.int32, sc.shape, 0)
    key = lax.broadcasted_iota(jnp.int32, sc.shape, 1)
    masked = query == key
    sc = jnp.where(masked, lowest, sc)
    top = jnp.max(sc, axis=1, keepdims=True)
    expo = jnp.where(masked, 0.0, jnp.exp(sc - top))
    stat[0] = jnp.broadcast_to(top, stat.shape[1:])
    stat[1] = jnp.broadcast_to(jnp.sum(expo, axis=1, keepdims=True), stat.shape[1:])
    acc[...] = jnp.dot(expo.astype(jnp.bfloat16), kk, preferred_element_type=jnp.float32)

    def nth(k):
        return jnp.where(z == 0, blks - 1 - k, other_than(z, k))

    def z_block(k):
        return slot(nth(k), x)

    def x_block(k):
        return slot(z, other_than(x, k))

    def far_block(i):
        return slot(nth(i // (tiles - 1)), other_than(x, lax.rem(i, tiles - 1)))

    far = (blks - 1) * (tiles - 1)
    repeat(0, blks - 1, lambda k: take(z_block(k), True))
    repeat(0, tiles - 1, lambda k: take(x_block(k), False))
    if blks == 4 and tiles == 2:
        attend(z_block(0), z_block(1))
        take(far_block(0), False)
        attend(z_block(2), x_block(0))
        take(far_block(1), False)
        attend(far_block(0))
        take(far_block(2), False)
        attend(far_block(1))
        attend(far_block(2))
    else:
        repeat(0, blks - 1, lambda k: attend(z_block(k)))
        repeat(0, tiles - 1, lambda k: attend(x_block(k)))
        take(far_block(0), False)

        def across(i):
            take(far_block(i), False)
            attend(far_block(i - 1))

        repeat(1, far, across)
        attend(far_block(far - 1))

    whole = both(mine).astype(jnp.float32)
    mixed = whole + acc[...] * (1.0 / stat[1][:, :1])
    squares = jnp.sum(mixed * mixed, axis=1, keepdims=True)
    wanted = jnp.where(s == 0, mixed[:, :width], mixed[:, width:])
    out_ref[...] = wanted * lax.rsqrt(squares + 1e-06)

    def home(k):
        @pl.when((k > 0) | (z < 2) | (z + 1 == blks))
        def _():
            left_home(k)

    repeat(0, blks - 1, home)
    every = keys.at[pl.ds(0, 2 * chips - blks)]
    pltpu.make_async_copy(every, every, sent).wait()


def local(raw_desc, desc_mean, whitening):
    rows, depth = raw_desc.shape
    width = whitening.shape[1]
    blks, tiles = lax.axis_size("blk"), lax.axis_size("tile")
    chips = blks * tiles
    vmem = pl.BlockSpec(memory_space=pltpu.VMEM)
    hbm = pl.BlockSpec(memory_space=pltpu.HBM)
    dma = pltpu.SemaphoreType.DMA
    bf16, f32 = jnp.bfloat16, jnp.float32
    raw_desc = pltpu.with_memory_space_constraint(raw_desc, pltpu.HBM)
    desc_mean = pltpu.with_memory_space_constraint(desc_mean, pltpu.HBM)
    whitening = pltpu.with_memory_space_constraint(whitening, pltpu.HBM)
    return pl.pallas_call(
        functools.partial(kernel, blks, tiles),
        out_shape=jax.ShapeDtypeStruct((rows, width), f32),
        in_specs=[hbm, hbm, hbm],
        out_specs=vmem,
        scratch_shapes=[
            pltpu.VMEM((rows, depth), bf16),
            pltpu.VMEM((depth,), f32),
            pltpu.VMEM((depth, width), bf16),
            pltpu.VMEM((2 * chips, rows, width), bf16),
            pltpu.VMEM((rows, 2 * width), f32),
            pltpu.VMEM((2, rows, width), f32),
            dma((slabs,)),
            dma((slabs,)),
            dma,
            dma,
            dma((chips, pieces)),
            dma((chips,)),
            pltpu.SemaphoreType.REGULAR((blks - 1,)),
            pltpu.SemaphoreType.REGULAR((tiles - 1,)),
            dma((blks - 1,)),
            pltpu.SemaphoreType.REGULAR,
        ],
        compiler_params=pltpu.CompilerParams(collective_id=0, has_side_effects=True, vmem_limit_bytes=40 * 2 ** 20),
        name="augment",
    )(raw_desc, desc_mean, whitening)


def solution(mesh):
    return jax.shard_map(
        local,
        mesh=mesh,
        in_specs=(P(("groups", "blk", "tile"), None), P(), P(None, "sub")),
        out_specs=P(("groups", "blk", "tile"), "sub"),
        check_vma=False,
    )
```

time: 19.3 us -> 17.5 us (0.907)
  the two profiles are of different devices: /device:TPU:0 before, /device:TPU:9 now
where the time goes in v1:
time: 17.5 us; the launch traced here: 17.3 us
  Pallas kernels  16.6 us (95%)
  local copies, waits for them, and re-layouts  0.66 us (4%)
    pallas_call x1, Pallas kernels, local(): pl.pallas_call(functools.partial(kernel, blks, tiles), out_shape=jax.Shap...  16.6 us
    unnamed x1, local copies, waits for them, and re-layouts  0.66 us

profile of v1, /device:TPU:9, one launch (start us, length us, event | category | flops | bytes accessed | tf_op | source)
XLA Modules:
  0.0 17.3 jit_solution(12247378131326729141)
XLA Ops:
  0.0 16.6 %augment.1 = f32[256,128]{1,0:T(8,128)S(1)} custom-call(bf16[256,1536]{1,0:T(8,128)(2,1)} %raw_hbm.1, f32[1536]{0:T(1024)} %mean_hbm.1, bf16[1536,128]{1,0:T(8,128)(2,1)} %white_hbm.1), custom_call_target="tpu_custom_call" | custom-call | tf_op jit(solution)/shard_map/augment/pallas_call | solution.py:282
  16.7 0.7 %copy.5 = f32[256,128]{1,0:T(8,128)} copy(f32[256,128]{1,0:T(8,128)S(1)} %augment.1) | data formatting | bytes 262144

commit v2 on v1

--- a/solution.py
+++ b/solution.py
@@ -29,8 +29,8 @@
 def kernel(
     blks, tiles,
     raw_hbm, mean_hbm, white_hbm, out_ref,
-    raw, mean, white, keys, acc, stat,
-    raw_sem, white_sem, mean_sem, sent, recv, pair_recv, ready_z, ready_x, gone, token,
+    raw, mean, white, keys, query, feats, acc, best, total,
+    raw_sem, white_sem, mean_sem, sent, recv, pair_recv, ready_z, ready_x, gone, turn, token,
 ):
     z, x, s = lax.axis_index("blk"), lax.axis_index("tile"), lax.axis_index("sub")
     other = 1 - s
@@ -100,8 +100,9 @@
             at, at, done, recv.at[block, p], device_id=device, device_id_type=MESH,
         ).start()
 
-    def left_home(k):
-        pltpu.make_async_copy(keys.at[0], keys.at[0], gone.at[k]).wait()
+    def left_home(k, p):
+        at = keys.at[0, pl.ds(0, piece)]
+        pltpu.make_async_copy(at, at, gone.at[k, p]).wait()
 
     def share(block, p):
         at = keys.at[2 * block + s, pl.ds(p * piece, piece)]
@@ -121,7 +122,7 @@
     keys[2 * mine + s] = half.astype(jnp.bfloat16)
     def push(k):
         for p in range(pieces):
-            send(mine, p, to_z(k), gone.at[k])
+            send(mine, p, to_z(k), gone.at[k, p])
 
     def rightward(k):
         @pl.when(k >= z)
@@ -148,20 +149,22 @@
     def _():
         push(0)
 
+    repeat(0, tiles - 1, sideward)
+    repeat(0, blks - 1, rightward)
+
     @pl.when(z > 1)
     def _():
+        left_home(0, 0)
+        pl.semaphore_signal(turn, inc=1, device_id={"sub": other}, device_id_type=MESH)
+
+        @pl.when(z + 1 < blks)
+        def _():
+            for r in range(2):
+                pl.semaphore_signal(
+                    token, inc=1, device_id={"blk": z + 1, "sub": r}, device_id_type=MESH,
+                )
+        pl.semaphore_wait(turn, 1)
         push(z - 1)
-
-    repeat(0, tiles - 1, sideward)
-    repeat(0, blks - 1, rightward)
-
-    @pl.when((z > 1) & (z + 1 < blks))
-    def _():
-        left_home(0)
-        for r in range(2):
-            pl.semaphore_signal(
-                token, inc=1, device_id={"blk": z + 1, "sub": r}, device_id_type=MESH,
-            )
 
     @pl.when(z > 2)
     def _():
@@ -184,42 +187,56 @@
         pltpu.make_async_copy(at, at, pair_recv.at[block]).wait()
 
     def scores_of(kk):
-        nt = (((1,), (1,)), ((), ()))
-        return beta * lax.dot_general(both(mine), kk, nt, preferred_element_type=jnp.float32)
+        return jnp.dot(kk, query[...], preferred_element_type=jnp.float32)
+
+    def weigh(kk, expo):
+        tn = (((0,), (0,)), ((), ()))
+        return lax.dot_general(
+            kk, expo.astype(jnp.bfloat16), tn, preferred_element_type=jnp.float32
+        )
+
+    def folded(values):
+        return jnp.sum(values.reshape(-1, 8, values.shape[1]), axis=0)
 
     def attend(*blocks):
         for block in blocks:
             paired(block)
         kk = jnp.concatenate([both(block) for block in blocks], axis=0)
         sc = scores_of(kk)
-        old = stat[0]
-        top = jnp.maximum(old, jnp.max(sc, axis=1, keepdims=True))
+        old = best[...]
+        top = jnp.maximum(old, jnp.max(sc, axis=0, keepdims=True))
         scale = jnp.exp(old - top)
-        expo = jnp.exp(sc - top[:, :1])
-        stat[0] = top
-        stat[1] = stat[1] * scale + jnp.sum(expo, axis=1, keepdims=True)
-        acc[...] = acc[...] * scale[:, :1] + jnp.dot(
-            expo.astype(jnp.bfloat16), kk, preferred_element_type=jnp.float32
-        )
+        expo = jnp.exp(sc - top)
+        best[...] = top
+        total[...] = total[...] * scale + folded(expo)
+        acc[...] = acc[...] * scale + weigh(kk, expo)
 
     paired(mine)
-    kk = both(mine)
-    sc = scores_of(kk)
-    query = lax.broadcasted_iota(jnp.int32, sc.shape, 0)
-    key = lax.broadcasted_iota(jnp.int32, sc.shape, 1)
-    masked = query == key
+    own = both(mine)
+    turned = own.astype(jnp.float32).T
+    feats[...] = turned
+    query[...] = (turned * beta).astype(jnp.bfloat16)
+    sc = scores_of(own)
+    key_at = lax.broadcasted_iota(jnp.int32, sc.shape, 0)
+    query_at = lax.broadcasted_iota(jnp.int32, sc.shape, 1)
+    masked = query_at == key_at
     sc = jnp.where(masked, lowest, sc)
-    top = jnp.max(sc, axis=1, keepdims=True)
+    top = jnp.max(sc, axis=0, keepdims=True)
     expo = jnp.where(masked, 0.0, jnp.exp(sc - top))
-    stat[0] = jnp.broadcast_to(top, stat.shape[1:])
-    stat[1] = jnp.broadcast_to(jnp.sum(expo, axis=1, keepdims=True), stat.shape[1:])
-    acc[...] = jnp.dot(expo.astype(jnp.bfloat16), kk, preferred_element_type=jnp.float32)
+    best[...] = top
+    total[...] = folded(expo)
+    acc[...] = weigh(own, expo)
 
     def nth(k):
-        return jnp.where(z == 0, blks - 1 - k, other_than(z, k))
+        near = lax.rem(k + blks - 2, blks - 1)
+        ahead = jnp.where(z == blks - 1, near, other_than(z, k))
+        return jnp.where(z == 0, blks - 1 - k, ahead)
 
     def z_block(k):
-        return slot(nth(k), x)
+        back = (z == 0) & (s == 0)
+        near = lax.rem(k + blks - 2, blks - 1)
+        ahead = jnp.where(z == blks - 1, near, other_than(z, k))
+        return slot(jnp.where(back, blks - 1 - k, ahead), x)
 
     def x_block(k):
         return slot(z, other_than(x, k))
@@ -231,13 +248,12 @@
     repeat(0, blks - 1, lambda k: take(z_block(k), True))
     repeat(0, tiles - 1, lambda k: take(x_block(k), False))
     if blks == 4 and tiles == 2:
-        attend(z_block(0), z_block(1))
+        attend(slot(nth(0), x), slot(nth(1), x))
+        attend(slot(nth(2), x), x_block(0))
         take(far_block(0), False)
-        attend(z_block(2), x_block(0))
         take(far_block(1), False)
-        attend(far_block(0))
         take(far_block(2), False)
-        attend(far_block(1))
+        attend(far_block(0), far_block(1))
         attend(far_block(2))
     else:
         repeat(0, blks - 1, lambda k: attend(z_block(k)))
@@ -251,16 +267,17 @@
         repeat(1, far, across)
         attend(far_block(far - 1))
 
-    whole = both(mine).astype(jnp.float32)
-    mixed = whole + acc[...] * (1.0 / stat[1][:, :1])
-    squares = jnp.sum(mixed * mixed, axis=1, keepdims=True)
-    wanted = jnp.where(s == 0, mixed[:, :width], mixed[:, width:])
-    out_ref[...] = wanted * lax.rsqrt(squares + 1e-06)
+    mixed = feats[...] + acc[...] * (1.0 / jnp.sum(total[...], axis=0, keepdims=True))
+    squares = jnp.sum(mixed * mixed, axis=0, keepdims=True)
+    wanted = jnp.where(s == 0, mixed[:width], mixed[width:])
+    out_ref[...] = (wanted * lax.rsqrt(squares + 1e-06)).T
 
     def home(k):
-        @pl.when((k > 0) | (z < 2) | (z + 1 == blks))
-        def _():
-            left_home(k)
+        @pl.when((k > 0) | (z < 2))
+        def _():
+            left_home(k, 0)
+        for p in range(1, pieces):
+            left_home(k, p)
 
     repeat(0, blks - 1, home)
     every = keys.at[pl.ds(0, 2 * chips - blks)]
@@ -289,8 +306,11 @@
             pltpu.VMEM((depth,), f32),
             pltpu.VMEM((depth, width), bf16),
             pltpu.VMEM((2 * chips, rows, width), bf16),
-            pltpu.VMEM((rows, 2 * width), f32),
-            pltpu.VMEM((2, rows, width), f32),
+            pltpu.VMEM((2 * width, rows), bf16),
+            pltpu.VMEM((2 * width, rows), f32),
+            pltpu.VMEM((2 * width, rows), f32),
+            pltpu.VMEM((1, rows), f32),
+            pltpu.VMEM((8, rows), f32),
             dma((slabs,)),
             dma((slabs,)),
             dma,
@@ -299,7 +319,8 @@
             dma((chips,)),
             pltpu.SemaphoreType.REGULAR((blks - 1,)),
             pltpu.SemaphoreType.REGULAR((tiles - 1,)),
-            dma((blks - 1,)),
+            dma((blks - 1, pieces)),
+            pltpu.SemaphoreType.REGULAR,
             pltpu.SemaphoreType.REGULAR,
         ],
         compiler_params=pltpu.CompilerParams(collective_id=0, has_side_effects=True, vmem_limit_bytes=40 * 2 ** 20),

time: 17.5 us -> 16.6 us (0.949)
  Pallas kernels: 16.6 us -> 15.8 us
    pallas_call x1, Pallas kernels: 16.6 us -> 15.8 us  [local(): pl.pallas_call(functools.partial(kernel, blks, tiles), out_shape=jax.Shap...]
where the time goes in v2:
time: 16.6 us; the launch traced here: 16.5 us
  Pallas kernels  15.8 us (95%)
  local copies, waits for them, and re-layouts  0.66 us (4%)
    pallas_call x1, Pallas kernels, local(): pl.pallas_call(functools.partial(kernel, blks, tiles), out_shape=jax.Shap...  15.8 us
    unnamed x1, local copies, waits for them, and re-layouts  0.66 us

profile of v2, /device:TPU:9, one launch (start us, length us, event | category | flops | bytes accessed | tf_op | source)
XLA Modules:
  0.0 16.5 jit_solution(14736509059235978447)
XLA Ops:
  0.0 15.8 %augment.1 = f32[256,128]{1,0:T(8,128)S(1)} custom-call(bf16[256,1536]{1,0:T(8,128)(2,1)} %raw_hbm.1, f32[1536]{0:T(1024)} %mean_hbm.1, bf16[1536,128]{1,0:T(8,128)(2,1)} %white_hbm.1), custom_call_target="tpu_custom_call" | custom-call | tf_op jit(solution)/shard_map/augment/pallas_call | solution.py:299
  15.8 0.7 %copy.5 = f32[256,128]{1,0:T(8,128)} copy(f32[256,128]{1,0:T(8,128)S(1)} %augment.1) | data formatting | bytes 262144

commit v3 on v2

v3 whole, which is shorter than its diff:
```python
import functools

import jax
import jax.numpy as jnp
from jax import lax
from jax.experimental import pallas as pl
from jax.experimental.pallas import tpu as pltpu
from jax.sharding import PartitionSpec as P

beta = 0.125
lowest = -1e30
slabs = 2
MESH = pl.DeviceIdType.MESH


def repeat(start, stop, body):
    if stop - start <= 8:
        for k in range(start, stop):
            body(k)
    else:
        lax.fori_loop(start, stop, lambda k, _: (body(k), 0)[1], 0)


def other_than(me, k):
    return k + jnp.where(k >= me, 1, 0)


def place(who, me):
    return who - jnp.where(who > me, 1, 0)


def kernel(
    blks, tiles,
    raw_hbm, mean_hbm, white_hbm, out_ref,
    raw, mean, white, keys, query, feats, acc, best, total,
    raw_sem, white_sem, mean_sem, sent, gone, recv, late, pair_recv, ready_z, ready_x, turn,
):
    z, x, s = lax.axis_index("blk"), lax.axis_index("tile"), lax.axis_index("sub")
    other = 1 - s
    rows, width = keys.shape[1], keys.shape[2]
    chips = blks * tiles
    piece = rows // 2
    slab = raw.shape[1] // slabs
    loads = []
    for c in range(slabs):
        at = pl.ds(c * slab, slab)
        loads.append(pltpu.make_async_copy(raw_hbm.at[:, at], raw.at[:, at], raw_sem.at[c]))
        loads[-1].start()
        if c == 0:
            load_mean = pltpu.make_async_copy(mean_hbm, mean, mean_sem)
            load_mean.start()
            load_white = pltpu.make_async_copy(white_hbm, white, white_sem)
            load_white.start()

    barrier = pltpu.get_barrier_semaphore()

    def signal(sem, device):
        pl.semaphore_signal(sem, inc=1, device_id=device, device_id_type=MESH)

    def to_z(k):
        return {"blk": other_than(z, k)}

    def to_x(k):
        return {"tile": other_than(x, k)}

    def greet_z(k):
        @pl.when(k >= z)
        def _():
            signal(barrier, to_z(k))

    def greet_x(k):
        @pl.when(k >= x)
        def _():
            signal(barrier, to_x(k))

    def answer_z(k):
        @pl.when(k < z)
        def _():
            signal(ready_z.at[z - 1], to_z(k))

    def answer_x(k):
        @pl.when(k < x)
        def _():
            signal(ready_x.at[x - 1], to_x(k))

    signal(barrier, {"sub": other})
    repeat(0, blks - 1, greet_z)
    repeat(0, tiles - 1, greet_x)
    pl.semaphore_wait(barrier, 1 + z + x)
    repeat(0, blks - 1, answer_z)
    repeat(0, tiles - 1, answer_x)

    def slot(zz, xx):
        return zz * tiles + xx

    mine = slot(z, x)

    def copy_to(at, done, arrived, device):
        pltpu.make_async_remote_copy(
            at, at, done, arrived, device_id=device, device_id_type=MESH,
        ).start()

    def part(block, p):
        return keys.at[2 * block + s, pl.ds(p * piece, piece)]

    def half(block):
        return keys.at[2 * block + s]

    def landed(at, sem):
        pltpu.make_async_copy(at, at, sem).wait()

    def centre(c):
        at = pl.ds(c * slab, slab)
        return (raw[:, at].astype(jnp.float32) - mean[at].reshape(1, -1)).astype(jnp.bfloat16)

    for c in range(slabs):
        loads[c].wait()
        if c == 0:
            load_mean.wait()
        if c == slabs - 1:
            load_white.wait()
        raw[:, pl.ds(c * slab, slab)] = centre(c)
    keys[2 * mine + s] = jnp.dot(
        raw[...], white[...], preferred_element_type=jnp.float32
    ).astype(jnp.bfloat16)

    def push(k, done=sent):
        dest = other_than(z, k)
        copy_to(part(mine, 0), done, recv.at[mine], {"blk": dest})
        copy_to(part(mine, 1), sent, late.at[place(z, dest)], {"blk": dest})

    def rightward(k):
        @pl.when(k >= z)
        def _():
            pl.semaphore_wait(ready_z.at[k], 1)
            push(k)

    def leftward(k):
        @pl.when(k < z - 1)
        def _():
            push(k)

    def sideward(k):
        @pl.when(k >= x)
        def _():
            pl.semaphore_wait(ready_x.at[k], 1)
        copy_to(half(mine), sent, recv.at[mine], to_x(k))

    for p in range(2):
        copy_to(part(mine, p), sent if p else gone, recv.at[mine], {"sub": other})

    @pl.when(z > 0)
    def _():
        push(0, gone)

    repeat(0, tiles - 1, sideward)

    @pl.when(z == 0)
    def _():
        pl.semaphore_wait(ready_z.at[0], 1)
        push(0, gone)

    repeat(1, blks - 1, rightward)

    @pl.when(z > 1)
    def _():
        landed(half(0), gone)
        signal(turn, {"sub": other})

        @pl.when(z + 1 < blks)
        def _():
            for r in range(2):
                signal(turn, {"blk": z + 1, "sub": r})
        pl.semaphore_wait(turn, jnp.where(z > 2, 3, 1))
        repeat(1, blks - 1, leftward)
        push(z - 1)

    def share(block, group):
        copy_to(half(block), sent, pair_recv.at[group], {"sub": other})

    def take_z(block, zz, group):
        for p in range(2):
            landed(part(block, p), late.at[place(zz, z)] if p else recv.at[block])
            repeat(0, tiles - 1, lambda k: copy_to(part(block, p), sent, recv.at[block], to_x(k)))
        share(block, group)

    def take(block, group):
        landed(half(block), recv.at[block])
        share(block, group)

    def both(block):
        return jnp.concatenate([keys[2 * block], keys[2 * block + 1]], axis=1)

    def paired(count, group):
        landed(keys.at[pl.ds(0, count)], pair_recv.at[group])

    def scores_of(kk):
        return jnp.dot(kk, query[...], preferred_element_type=jnp.float32)

    def weigh(kk, expo):
        tn = (((0,), (0,)), ((), ()))
        return lax.dot_general(
            kk, expo.astype(jnp.bfloat16), tn, preferred_element_type=jnp.float32
        )

    def folded(values):
        return jnp.sum(values.reshape(-1, 8, values.shape[1]), axis=0)

    def attend(*blocks):
        kk = jnp.concatenate([both(block) for block in blocks], axis=0)
        sc = scores_of(kk)
        old = best[...]
        top = jnp.maximum(old, jnp.max(sc, axis=0, keepdims=True))
        scale = jnp.exp(old - top)
        expo = jnp.exp(sc - top)
        best[...] = top
        total[...] = total[...] * scale + folded(expo)
        acc[...] = acc[...] * scale + weigh(kk, expo)

    landed(keys.at[2 * mine + other], recv.at[mine])
    own = both(mine)
    turned = own.astype(jnp.float32).T
    feats[...] = turned
    query[...] = (turned * beta).astype(jnp.bfloat16)
    sc = scores_of(own)
    key_at = lax.broadcasted_iota(jnp.int32, sc.shape, 0)
    query_at = lax.broadcasted_iota(jnp.int32, sc.shape, 1)
    masked = query_at == key_at
    sc = jnp.where(masked, lowest, sc)
    top = jnp.max(sc, axis=0, keepdims=True)
    expo = jnp.where(masked, 0.0, jnp.exp(sc - top))
    best[...] = top
    total[...] = folded(expo)
    acc[...] = weigh(own, expo)

    def nth(k):
        near = lax.rem(k + blks - 2, blks - 1)
        ahead = jnp.where(z == blks - 1, near, other_than(z, k))
        ahead = jnp.where((z == 1) & (k > 0), blks - k, ahead)
        return jnp.where(z == 0, blks - 1 - k, ahead)

    def z_take(k):
        zz = jnp.where((z == 0) & (s == 1), k + 1, nth(k))
        take_z(slot(zz, x), zz, 0)

    def x_block(k):
        return slot(z, other_than(x, k))

    def far_block(i):
        return slot(nth(i // (tiles - 1)), other_than(x, lax.rem(i, tiles - 1)))

    far = (blks - 1) * (tiles - 1)
    repeat(0, blks - 1, z_take)
    repeat(0, tiles - 1, lambda k: take(x_block(k), 0))
    if blks == 4 and tiles == 2:
        paired(4, 0)
        attend(*[slot(nth(k), x) for k in range(3)], x_block(0))
        take(far_block(0), 1)
        take(far_block(1), 1)
        take(far_block(2), 2)
        paired(2, 1)
        attend(far_block(0), far_block(1))
        paired(1, 2)
        attend(far_block(2))
    else:
        repeat(0, far, lambda i: take(far_block(i), 0))
        paired(chips - 1, 0)
        repeat(0, blks - 1, lambda k: attend(slot(nth(k), x)))
        repeat(0, tiles - 1, lambda k: attend(x_block(k)))
        repeat(0, far, lambda i: attend(far_block(i)))

    mixed = feats[...] + acc[...] * (1.0 / jnp.sum(total[...], axis=0, keepdims=True))
    squares = jnp.sum(mixed * mixed, axis=0, keepdims=True)
    wanted = jnp.where(s == 0, mixed[:width], mixed[width:])
    out_ref[...] = (wanted * lax.rsqrt(squares + 1e-06)).T

    @pl.when(z < 2)
    def _():
        landed(half(0), gone)
    landed(keys.at[pl.ds(0, 2 * chips - 2)], sent)


def local(raw_desc, desc_mean, whitening):
    rows, depth = raw_desc.shape
    width = whitening.shape[1]
    blks, tiles = lax.axis_size("blk"), lax.axis_size("tile")
    chips = blks * tiles
    vmem = pl.BlockSpec(memory_space=pltpu.VMEM)
    hbm = pl.BlockSpec(memory_space=pltpu.HBM)
    dma = pltpu.SemaphoreType.DMA
    regular = pltpu.SemaphoreType.REGULAR
    bf16, f32 = jnp.bfloat16, jnp.float32
    raw_desc = pltpu.with_memory_space_constraint(raw_desc, pltpu.HBM)
    desc_mean = pltpu.with_memory_space_constraint(desc_mean, pltpu.HBM)
    whitening = pltpu.with_memory_space_constraint(whitening, pltpu.HBM)
    return pl.pallas_call(
        functools.partial(kernel, blks, tiles),
        out_shape=jax.ShapeDtypeStruct((rows, width), f32),
        in_specs=[hbm, hbm, hbm],
        out_specs=vmem,
        scratch_shapes=[
            pltpu.VMEM((rows, depth), bf16),
            pltpu.VMEM((depth,), f32),
            pltpu.VMEM((depth, width), bf16),
            pltpu.VMEM((2 * chips, rows, width), bf16),
            pltpu.VMEM((2 * width, rows), bf16),
            pltpu.VMEM((2 * width, rows), f32),
            pltpu.VMEM((2 * width, rows), f32),
            pltpu.VMEM((1, rows), f32),
            pltpu.VMEM((8, rows), f32),
            dma((slabs,)),
            dma,
            dma,
            dma,
            dma,
            dma((chips,)),
            dma((blks - 1,)),
            dma((3,)),
            regular((blks - 1,)),
            regular((tiles - 1,)),
            regular,
        ],
        compiler_params=pltpu.CompilerParams(collective_id=0, has_side_effects=True, vmem_limit_bytes=40 * 2 ** 20),
        name="augment",
    )(raw_desc, desc_mean, whitening)


def solution(mesh):
    return jax.shard_map(
        local,
        mesh=mesh,
        in_specs=(P(("groups", "blk", "tile"), None), P(), P(None, "sub")),
        out_specs=P(("groups", "blk", "tile"), "sub"),
        check_vma=False,
    )
```

time: 16.6 us -> 16.3 us (0.982)
  Pallas kernels: 15.8 us -> 15.5 us
    pallas_call x1, Pallas kernels: 15.8 us -> 15.5 us  [local(): pl.pallas_call(functools.partial(kernel, blks, tiles), out_shape=jax.Shap...]
where the time goes in v3:
time: 16.3 us; the launch traced here: 16.2 us
  Pallas kernels  15.5 us (95%)
  local copies, waits for them, and re-layouts  0.66 us (4%)
    pallas_call x1, Pallas kernels, local(): pl.pallas_call(functools.partial(kernel, blks, tiles), out_shape=jax.Shap...  15.5 us
    unnamed x1, local copies, waits for them, and re-layouts  0.66 us

profile of v3, /device:TPU:9, one launch (start us, length us, event | category | flops | bytes accessed | tf_op | source)
XLA Modules:
  0.0 16.2 jit_solution(16528577076670223228)
XLA Ops:
  0.0 15.5 %augment.1 = f32[256,128]{1,0:T(8,128)S(1)} custom-call(bf16[256,1536]{1,0:T(8,128)(2,1)} %raw_hbm.1, f32[1536]{0:T(1024)} %mean_hbm.1, bf16[1536,128]{1,0:T(8,128)(2,1)} %white_hbm.1), custom_call_target="tpu_custom_call" | custom-call | tf_op jit(solution)/shard_map/augment/pallas_call | solution.py:296
  15.5 0.7 %copy.5 = f32[256,128]{1,0:T(8,128)} copy(f32[256,128]{1,0:T(8,128)S(1)} %augment.1) | data formatting | bytes 262144

commit v4 on v3

--- a/solution.py
+++ b/solution.py
@@ -33,12 +33,13 @@
     blks, tiles,
     raw_hbm, mean_hbm, white_hbm, out_ref,
     raw, mean, white, keys, query, feats, acc, best, total,
-    raw_sem, white_sem, mean_sem, sent, gone, recv, late, pair_recv, ready_z, ready_x, turn,
+    raw_sem, white_sem, mean_sem, sent, gone, recv, late, pair_recv, ready_z, ready_x, turn, last,
 ):
     z, x, s = lax.axis_index("blk"), lax.axis_index("tile"), lax.axis_index("sub")
     other = 1 - s
     rows, width = keys.shape[1], keys.shape[2]
     chips = blks * tiles
+    paired_up = blks == 4 and tiles == 2
     piece = rows // 2
     slab = raw.shape[1] // slabs
     loads = []
@@ -136,7 +137,9 @@
             push(k)
 
     def leftward(k):
-        @pl.when(k < z - 1)
+        direct = (k < z - 1) & jnp.logical_not(paired_up & (s == 1))
+
+        @pl.when(direct)
         def _():
             push(k)
 
@@ -178,11 +181,38 @@
     def share(block, group):
         copy_to(half(block), sent, pair_recv.at[group], {"sub": other})
 
+    def relay(block, zz, p):
+        at = part(block, p)
+        if not paired_up or p == 0:
+            repeat(0, tiles - 1, lambda k: copy_to(at, sent, recv.at[block], to_x(k)))
+            return
+        final = zz == nth(blks - 2)
+
+        @pl.when(final)
+        def _():
+            copy_to(at, sent, last, to_x(0))
+            copy_to(at, sent, pair_recv.at[2], {"tile": other_than(x, 0), "sub": other})
+
+        @pl.when(jnp.logical_not(final))
+        def _():
+            copy_to(at, sent, recv.at[block], to_x(0))
+
     def take_z(block, zz, group):
         for p in range(2):
             landed(part(block, p), late.at[place(zz, z)] if p else recv.at[block])
-            repeat(0, tiles - 1, lambda k: copy_to(part(block, p), sent, recv.at[block], to_x(k)))
+            relay(block, zz, p)
+            if paired_up:
+                arrived = late.at[place(zz, 1)] if p else recv.at[block]
+
+                @pl.when((z == 0) & (s == 1) & (zz == blks - 1))
+                def _():
+                    copy_to(part(block, p), sent, arrived, {"blk": 1})
         share(block, group)
+
+    def take_last(block):
+        landed(part(block, 0), recv.at[block])
+        copy_to(part(block, 0), sent, pair_recv.at[2], {"sub": other})
+        landed(part(block, 1), last)
 
     def take(block, group):
         landed(half(block), recv.at[block])
@@ -240,7 +270,7 @@
         return jnp.where(z == 0, blks - 1 - k, ahead)
 
     def z_take(k):
-        zz = jnp.where((z == 0) & (s == 1), k + 1, nth(k))
+        zz = jnp.where((z <= 1) & (s == 1), other_than(z, k), nth(k))
         take_z(slot(zz, x), zz, 0)
 
     def x_block(k):
@@ -252,16 +282,33 @@
     far = (blks - 1) * (tiles - 1)
     repeat(0, blks - 1, z_take)
     repeat(0, tiles - 1, lambda k: take(x_block(k), 0))
-    if blks == 4 and tiles == 2:
-        paired(4, 0)
-        attend(*[slot(nth(k), x) for k in range(3)], x_block(0))
-        take(far_block(0), 1)
-        take(far_block(1), 1)
-        take(far_block(2), 2)
-        paired(2, 1)
-        attend(far_block(0), far_block(1))
-        paired(1, 2)
-        attend(far_block(2))
+    if paired_up:
+        def near_ones():
+            paired(4, 0)
+            attend(*[slot(nth(k), x) for k in range(3)], x_block(0))
+
+        def first_far():
+            paired(1, 1)
+            attend(far_block(0))
+
+        @pl.when(s == 0)
+        def _():
+            near_ones()
+            take(far_block(0), 1)
+            first_far()
+            take(far_block(1), 2)
+            take_last(far_block(2))
+
+        @pl.when(s == 1)
+        def _():
+            take(far_block(0), 1)
+            near_ones()
+            take(far_block(1), 2)
+            take_last(far_block(2))
+            first_far()
+
+        paired(2, 2)
+        attend(far_block(1), far_block(2))
     else:
         repeat(0, far, lambda i: take(far_block(i), 0))
         paired(chips - 1, 0)
@@ -277,7 +324,24 @@
     @pl.when(z < 2)
     def _():
         landed(half(0), gone)
-    landed(keys.at[pl.ds(0, 2 * chips - 2)], sent)
+    units = 2 * chips - 2
+    if paired_up:
+        more = (z == 0) & (s == 1)
+        fewer = (z == blks - 1) & (s == 1)
+
+        @pl.when(more)
+        def _():
+            landed(keys.at[pl.ds(0, units + 1)], sent)
+
+        @pl.when(fewer)
+        def _():
+            landed(keys.at[pl.ds(0, units - 1)], sent)
+
+        @pl.when(jnp.logical_not(more | fewer))
+        def _():
+            landed(keys.at[pl.ds(0, units)], sent)
+    else:
+        landed(keys.at[pl.ds(0, units)], sent)
 
 
 def local(raw_desc, desc_mean, whitening):
@@ -319,6 +383,7 @@
             regular((blks - 1,)),
             regular((tiles - 1,)),
             regular,
+            dma,
         ],
         compiler_params=pltpu.CompilerParams(collective_id=0, has_side_effects=True, vmem_limit_bytes=40 * 2 ** 20),
         name="augment",

time: 16.3 us -> 16 us (0.982)
  Pallas kernels: 15.5 us -> 15.2 us
    pallas_call x1, Pallas kernels: 15.5 us -> 15.2 us  [local(): pl.pallas_call(functools.partial(kernel, blks, tiles), out_shape=jax.Shap...]
where the time goes in v4:
time: 16 us; the launch traced here: 15.8 us
  Pallas kernels  15.2 us (95%)
  local copies, waits for them, and re-layouts  0.66 us (4%)
    pallas_call x1, Pallas kernels, local(): pl.pallas_call(functools.partial(kernel, blks, tiles), out_shape=jax.Shap...  15.2 us
    unnamed x1, local copies, waits for them, and re-layouts  0.66 us

profile of v4, /device:TPU:9, one launch (start us, length us, event | category | flops | bytes accessed | tf_op | source)
XLA Modules:
  0.0 15.8 jit_solution(2366640453833262091)
XLA Ops:
  0.0 15.2 %augment.1 = f32[256,128]{1,0:T(8,128)S(1)} custom-call(bf16[256,1536]{1,0:T(8,128)(2,1)} %raw_hbm.1, f32[1536]{0:T(1024)} %mean_hbm.1, bf16[1536,128]{1,0:T(8,128)(2,1)} %white_hbm.1), custom_call_target="tpu_custom_call" | custom-call | tf_op jit(solution)/shard_map/augment/pallas_call | solution.py:360
  15.2 0.7 %copy.5 = f32[256,128]{1,0:T(8,128)} copy(f32[256,128]{1,0:T(8,128)S(1)} %augment.1) | data formatting | bytes 262144

commit v5 on v4

--- a/solution.py
+++ b/solution.py
@@ -41,6 +41,7 @@
     chips = blks * tiles
     paired_up = blks == 4 and tiles == 2
     piece = rows // 2
+    cut = rows // 4
     slab = raw.shape[1] // slabs
     loads = []
     for c in range(slabs):
@@ -107,6 +108,10 @@
     def half(block):
         return keys.at[2 * block + s]
 
+    def ends(block):
+        at = keys.at[2 * block + s]
+        return at.at[pl.ds(0, cut)], at.at[pl.ds(cut, rows - cut)]
+
     def landed(at, sem):
         pltpu.make_async_copy(at, at, sem).wait()
 
@@ -183,15 +188,20 @@
 
     def relay(block, zz, p):
         at = part(block, p)
-        if not paired_up or p == 0:
+        if not paired_up:
             repeat(0, tiles - 1, lambda k: copy_to(at, sent, recv.at[block], to_x(k)))
             return
-        final = zz == nth(blks - 2)
+        final = (zz == nth(blks - 2)) & (s == 0)
+        first, rest = ends(block)
 
         @pl.when(final)
         def _():
-            copy_to(at, sent, last, to_x(0))
-            copy_to(at, sent, pair_recv.at[2], {"tile": other_than(x, 0), "sub": other})
+            if p == 0:
+                copy_to(first, sent, recv.at[block], to_x(0))
+            else:
+                copy_to(rest, sent, last, to_x(0))
+                across = {"tile": other_than(x, 0), "sub": other}
+                copy_to(rest, sent, pair_recv.at[2], across)
 
         @pl.when(jnp.logical_not(final))
         def _():
@@ -210,9 +220,10 @@
         share(block, group)
 
     def take_last(block):
-        landed(part(block, 0), recv.at[block])
-        copy_to(part(block, 0), sent, pair_recv.at[2], {"sub": other})
-        landed(part(block, 1), last)
+        first, rest = ends(block)
+        landed(first, recv.at[block])
+        copy_to(first, sent, pair_recv.at[2], {"sub": other})
+        landed(rest, last)
 
     def take(block, group):
         landed(half(block), recv.at[block])
@@ -304,7 +315,7 @@
             take(far_block(0), 1)
             near_ones()
             take(far_block(1), 2)
-            take_last(far_block(2))
+            take(far_block(2), 2)
             first_far()
 
         paired(2, 2)

time: 16 us -> 15.8 us (0.988)
  the two profiles are of different devices: /device:TPU:9 before, /device:TPU:1 now
where the time goes in v5:
time: 15.8 us; the launch traced here: 15.6 us
  Pallas kernels  15 us (95%)
  local copies, waits for them, and re-layouts  0.66 us (4%)
    pallas_call x1, Pallas kernels, local(): pl.pallas_call(functools.partial(kernel, blks, tiles), out_shape=jax.Shap...  15 us
    unnamed x1, local copies, waits for them, and re-layouts  0.66 us

profile of v5, /device:TPU:1, one launch (start us, length us, event | category | flops | bytes accessed | tf_op | source)
XLA Modules:
  0.0 15.6 jit_solution(17712724850309594293)
XLA Ops:
  0.0 15.0 %augment.1 = f32[256,128]{1,0:T(8,128)S(1)} custom-call(bf16[256,1536]{1,0:T(8,128)(2,1)} %raw_hbm.1, f32[1536]{0:T(1024)} %mean_hbm.1, bf16[1536,128]{1,0:T(8,128)(2,1)} %white_hbm.1), custom_call_target="tpu_custom_call" | custom-call | tf_op jit(solution)/shard_map/augment/pallas_call | solution.py:371
  15.0 0.7 %copy.5 = f32[256,128]{1,0:T(8,128)} copy(f32[256,128]{1,0:T(8,128)S(1)} %augment.1) | data formatting | bytes 262144

commit v6 on v5

--- a/solution.py
+++ b/solution.py
@@ -85,10 +85,16 @@
         def _():
             signal(ready_x.at[x - 1], to_x(k))
 
+    corner = paired_up & (z == 1) & (x == 1) & (s == 0)
     signal(barrier, {"sub": other})
+
+    @pl.when(paired_up & (z == 0) & (x == 0) & (s == 0))
+    def _():
+        signal(barrier, {"blk": 1, "tile": 1 if paired_up else 0})
+
     repeat(0, blks - 1, greet_z)
     repeat(0, tiles - 1, greet_x)
-    pl.semaphore_wait(barrier, 1 + z + x)
+    pl.semaphore_wait(barrier, 1 + z + x + jnp.where(corner, 1, 0))
     repeat(0, blks - 1, answer_z)
     repeat(0, tiles - 1, answer_x)
 
@@ -161,6 +167,10 @@
     def _():
         push(0, gone)
 
+    @pl.when(corner)
+    def _():
+        copy_to(half(mine), sent, recv.at[mine], {"blk": 0, "tile": 0})
+
     repeat(0, tiles - 1, sideward)
 
     @pl.when(z == 0)
@@ -191,7 +201,8 @@
         if not paired_up:
             repeat(0, tiles - 1, lambda k: copy_to(at, sent, recv.at[block], to_x(k)))
             return
-        final = (zz == nth(blks - 2)) & (s == 0)
+        final = (zz == nth(blks - 2, other_than(x, 0))) & (s == 0)
+        spared = (z == 0) & (x == 1) & (s == 0)
         first, rest = ends(block)
 
         @pl.when(final)
@@ -203,7 +214,7 @@
                 across = {"tile": other_than(x, 0), "sub": other}
                 copy_to(rest, sent, pair_recv.at[2], across)
 
-        @pl.when(jnp.logical_not(final))
+        @pl.when(jnp.logical_not(final | (spared & (zz == 1))))
         def _():
             copy_to(at, sent, recv.at[block], to_x(0))
 
@@ -274,14 +285,17 @@
     total[...] = folded(expo)
     acc[...] = weigh(own, expo)
 
-    def nth(k):
+    def nth(k, xx=x):
         near = lax.rem(k + blks - 2, blks - 1)
         ahead = jnp.where(z == blks - 1, near, other_than(z, k))
         ahead = jnp.where((z == 1) & (k > 0), blks - k, ahead)
-        return jnp.where(z == 0, blks - 1 - k, ahead)
+        corner_first = jnp.where(k == 0, 1, blks - k)
+        down = blks - 1 - k
+        return jnp.where(z == 0, jnp.where(xx == 0, corner_first, down), ahead)
 
     def z_take(k):
-        zz = jnp.where((z <= 1) & (s == 1), other_than(z, k), nth(k))
+        back = jnp.where(z == 0, blks - 1 - k, nth(k))
+        zz = jnp.where((z <= 1) & (s == 1), other_than(z, k), back)
         take_z(slot(zz, x), zz, 0)
 
     def x_block(k):
@@ -337,8 +351,8 @@
         landed(half(0), gone)
     units = 2 * chips - 2
     if paired_up:
-        more = (z == 0) & (s == 1)
-        fewer = (z == blks - 1) & (s == 1)
+        more = ((z == 0) & (s == 1)) | corner
+        fewer = ((z == blks - 1) & (s == 1)) | ((z == 0) & (x == 1) & (s == 0))
 
         @pl.when(more)
         def _():

time: 15.8 us -> 15.4 us (0.975)
  the two profiles are of different devices: /device:TPU:1 before, /device:TPU:9 now
where the time goes in v6:
time: 15.4 us; the launch traced here: 15.3 us
  Pallas kernels  14.6 us (95%)
  local copies, waits for them, and re-layouts  0.66 us (4%)
    pallas_call x1, Pallas kernels, local(): pl.pallas_call(functools.partial(kernel, blks, tiles), out_shape=jax.Shap...  14.6 us
    unnamed x1, local copies, waits for them, and re-layouts  0.66 us

profile of v6, /device:TPU:9, one launch (start us, length us, event | category | flops | bytes accessed | tf_op | source)
XLA Modules:
  0.0 15.3 jit_solution(6559335585418079360)
XLA Ops:
  0.0 14.6 %augment.1 = f32[256,128]{1,0:T(8,128)S(1)} custom-call(bf16[256,1536]{1,0:T(8,128)(2,1)} %raw_hbm.1, f32[1536]{0:T(1024)} %mean_hbm.1, bf16[1536,128]{1,0:T(8,128)(2,1)} %white_hbm.1), custom_call_target="tpu_custom_call" | custom-call | tf_op jit(solution)/shard_map/augment/pallas_call | solution.py:385
  14.6 0.7 %copy.5 = f32[256,128]{1,0:T(8,128)} copy(f32[256,128]{1,0:T(8,128)S(1)} %augment.1) | data formatting | bytes 262144

commit v7 on v6

--- a/solution.py
+++ b/solution.py
@@ -183,13 +183,17 @@
     @pl.when(z > 1)
     def _():
         landed(half(0), gone)
-        signal(turn, {"sub": other})
+        @pl.when(z > 2)
+        def _():
+            signal(turn, {"sub": other})
 
         @pl.when(z + 1 < blks)
         def _():
             for r in range(2):
                 signal(turn, {"blk": z + 1, "sub": r})
-        pl.semaphore_wait(turn, jnp.where(z > 2, 3, 1))
+        @pl.when(z > 2)
+        def _():
+            pl.semaphore_wait(turn, 3)
         repeat(1, blks - 1, leftward)
         push(z - 1)
 

time: 15.4 us -> 15.4 us (level)
  no operation moved by 1% of the time
where the time goes in v7:
time: 15.4 us; the launch traced here: 15.3 us
  Pallas kernels  14.6 us (95%)
  local copies, waits for them, and re-layouts  0.66 us (4%)
    pallas_call x1, Pallas kernels, local(): pl.pallas_call(functools.partial(kernel, blks, tiles), out_shape=jax.Shap...  14.6 us
    unnamed x1, local copies, waits for them, and re-layouts  0.66 us

profile of v7, /device:TPU:9, one launch (start us, length us, event | category | flops | bytes accessed | tf_op | source)
XLA Modules:
  0.0 15.3 jit_solution(12351760033719969096)
XLA Ops:
  0.0 14.6 %augment.1 = f32[256,128]{1,0:T(8,128)S(1)} custom-call(bf16[256,1536]{1,0:T(8,128)(2,1)} %raw_hbm.1, f32[1536]{0:T(1024)} %mean_hbm.1, bf16[1536,128]{1,0:T(8,128)(2,1)} %white_hbm.1), custom_call_target="tpu_custom_call" | custom-call | tf_op jit(solution)/shard_map/augment/pallas_call | solution.py:389
  14.6 0.7 %copy.5 = f32[256,128]{1,0:T(8,128)} copy(f32[256,128]{1,0:T(8,128)S(1)} %augment.1) | data formatting | bytes 262144
